TPU v7x, 32 devices: a whole 2x2x4 slice. The times are simulated.
32 devices in a mesh: seq: 8 (over y, x, core), head: 4 (over z).
Axes of the slice: x: 2, y: 2, z: 4, core: 2. Of those that a mesh axis runs over, the one named last changes fastest.
Arguments:
- queries: bfloat16 [1536, 4096], P('seq', 'head'), may hold values from -1024 to 1024
- image_keys: bfloat16 [12808, 512], P('seq', 'head'), may hold values from -8 to 8
- image_values: bfloat16 [12808, 512], P('seq', 'head'), may hold values from -6 to 6
- layer_input: bfloat16 [1536, 8192], P('seq', 'head'), may hold values from -6 to 6
- out_weight: bfloat16 [4096, 8192], P('head'), may hold values from -0.125 to 0.125
- tile_counts: int32 [4], replicated, may hold values from 1 to 4, as said below
- image_range: int32 [2, 1536], P(None, 'seq'), may hold values from 0 to 4, as said below
- attn_gate: float32 [1], replicated, may hold values from 0.5 to 1.5
Outputs:
- layer_out: bfloat16 [1536, 8192], P('seq', 'head')
Inputs may be any that keep to these rules, and one draw needn't show every extreme that they name: `tile_counts`: each image has 1 to 4 tiles and together they have 8; some image has exactly 4. Images are numbered in text order. For every token t, image_range[0, t] <= image_range[1, t]; image_range[1, t] never decreases as t grows; image_range[1, 0] = 0, so tokens before the first image attend to none.
All inputs are finite; a program needn't handle non-finite values.
Results may differ from a plain program's by a relative error of at most 0.0055.
Values may be sent and summed in bfloat16 or wider, within the bound.
A program may use at most 512 MiB of HBM per device.

v0:
```python
import functools
import math

import jax
import jax.numpy as jnp
from jax import lax
from jax.experimental import pallas as pl
from jax.experimental.pallas import tpu as pltpu
from jax.sharding import PartitionSpec as P

MESH = pl.DeviceIdType.MESH
NEG = -1e30
BIG = 1e30
LANES = 128
PACK = 16


def round_up(value, unit):
    return -(-value // unit) * unit


def kernel(
    plan,
    counts_ref,
    q_ref,
    range_ref,
    kv_hbm,
    w_hbm,
    out_ref,
    kv,
    weight,
    run_max,
    total,
    numer,
    attended,
    term,
    sent,
    from_left,
    from_right,
    own_sem,
    weight_sem,
    kv_send,
    kv_recv,
    right_send,
    right_recv,
    left_send,
    left_recv,
):
    devices, heads, tile_rows, split, send_rows, images, chunks = plan
    square = devices == 8
    chips = devices // 2
    me = lax.axis_index("seq")
    h = lax.axis_index("head")
    core = lax.rem(me, 2)
    chip = me // 2
    partner = chip * 2 + (1 - core)
    rows, width = q_ref.shape
    head_dim = kv.shape[3]
    group = width // head_dim
    padded = kv.shape[2]
    columns = out_ref.shape[1]
    halves = ((0, split), (split, send_rows - split))

    def chip_at(offset):
        if square:
            cy, cx = chip // 2, lax.rem(chip, 2)
            oy, ox = offset // 2, lax.rem(offset, 2)
            return lax.rem(cy + oy, 2) * 2 + lax.rem(cx + ox, 2)
        return lax.rem(chip + offset, chips)

    def at(target):
        return (target, h)

    own = pltpu.make_async_copy(
        kv_hbm.at[:, pl.ds(0, send_rows), :], kv.at[me, :, pl.ds(0, send_rows), :], own_sem
    )
    own.start()
    fetch = pltpu.make_async_copy(w_hbm, weight, weight_sem)
    fetch.start()

    barrier = pltpu.get_barrier_semaphore()
    pl.semaphore_signal(barrier, inc=1, device_id=at(partner), device_id_type=MESH)
    for offset in range(1, chips):
        if square and offset == 3:
            continue
        pl.semaphore_signal(
            barrier, inc=1, device_id=at(chip_at(offset) * 2 + core), device_id_type=MESH
        )
    greeted = 1 + (2 if square else chips - 1)

    @pl.when(h > 0)
    def _():
        pl.semaphore_signal(barrier, inc=1, device_id=(me, h - 1), device_id_type=MESH)

    @pl.when(h < heads - 1)
    def _():
        pl.semaphore_signal(barrier, inc=1, device_id=(me, h + 1), device_id_type=MESH)

    ends = jnp.where(h > 0, 1, 0) + jnp.where(h < heads - 1, 1, 0)

    run_max[...] = jnp.full_like(run_max, NEG)
    total[...] = jnp.zeros_like(total)
    numer[...] = jnp.zeros_like(numer)
    if send_rows < padded:
        kv[:, :, send_rows:, :] = jnp.zeros(
            (devices, 2, padded - send_rows, head_dim), kv.dtype
        )
    pl.semaphore_wait(barrier, greeted + ends)
    own.wait()

    def kv_copy(slot, half, target, lane):
        start, size = halves[half]
        piece = kv.at[slot, :, pl.ds(start, size), :]
        return pltpu.make_async_remote_copy(
            src_ref=piece,
            dst_ref=piece,
            send_sem=kv_send.at[lane, half],
            recv_sem=kv_recv.at[slot, half],
            device_id=at(target),
            device_id_type=MESH,
        )

    def outgoing(offset, half):
        return kv_copy(me, half, chip_at(offset) * 2 + core, chips + offset)

    def to_partner(offset, half):
        return kv_copy(chip_at(offset) * 2 + core, half, partner, offset)

    def relay(half):
        source = 1 if half == 0 else 2
        return kv_copy(
            chip_at(source) * 2 + core, half, chip_at(3 - source) * 2 + core, chips + 3
        )

    if square:
        outgoing(1, 0).start()
        outgoing(2, 1).start()
        outgoing(1, 1).start()
        outgoing(2, 0).start()
    else:
        for offset in range(1, chips):
            for half in range(2):
                outgoing(offset, half).start()

    to_partner(0, 0).start()
    to_partner(0, 1).start()

    def image_of(slot):
        image, end = 0, 0
        for i in range(images):
            end = end + counts_ref[i]
            image = image + jnp.where(end <= slot, 1, 0)
        return image

    low = range_ref[:, 0:1]
    high = range_ref[:, 1:2]
    factor = math.log2(math.e) / math.sqrt(head_dim)
    last = padded - LANES
    real = tile_rows - last

    def lane_tiles(value):
        return [value[:, j : j + LANES] for j in range(0, value.shape[1], LANES)]

    def attend(slot_a, slot_b):
        image_a, image_b = image_of(slot_a), image_of(slot_b)
        ok_a = (low <= image_a) & (image_a < high)
        ok_b = (low <= image_b) & (image_b < high)

        def one_head(g):
            q = q_ref[:, pl.ds(pl.multiple_of(g * head_dim, head_dim), head_dim)]
            contract = (((1,), (1,)), ((), ()))
            s_a = lax.dot_general(
                q, kv[slot_a, 0, :split, :], contract, preferred_element_type=jnp.float32
            )
            s_b = lax.dot_general(
                q, kv[slot_b, 0, split:, :], contract, preferred_element_type=jnp.float32
            )
            edge = s_b[:, last - split :]
            lane = lax.broadcasted_iota(jnp.int32, edge.shape, 1)
            s_b = jnp.concatenate(
                [s_b[:, : last - split], jnp.where(lane < real, edge, NEG)], axis=1
            )
            top_a = jnp.max(functools.reduce(jnp.maximum, lane_tiles(s_a)), axis=1, keepdims=True)
            top_b = jnp.max(functools.reduce(jnp.maximum, lane_tiles(s_b)), axis=1, keepdims=True)
            old = run_max[g]
            new = jnp.maximum(
                old, jnp.maximum(jnp.where(ok_a, top_a, NEG), jnp.where(ok_b, top_b, NEG))
            )
            base_a = jnp.where(ok_a, new, BIG) * factor
            base_b = jnp.where(ok_b, new, BIG) * factor
            p_a = jnp.exp2(s_a * factor - base_a)
            p_b = jnp.exp2(s_b * factor - base_b)
            alpha = jnp.exp2((old - new) * factor)
            run_max[g] = new
            total[g] = total[g] * alpha + functools.reduce(
                jnp.add, lane_tiles(p_a) + lane_tiles(p_b)
            )
            mixed = jnp.dot(
                p_a.astype(jnp.bfloat16), kv[slot_a, 1, :split, :],
                preferred_element_type=jnp.float32,
            ) + jnp.dot(
                p_b.astype(jnp.bfloat16), kv[slot_b, 1, split:, :],
                preferred_element_type=jnp.float32,
            )
            numer[g] = numer[g] * alpha + mixed

        together = math.gcd(group, 4)

        def some_heads(block, carry):
            for k in range(together):
                one_head(block * together + k)
            return carry

        lax.fori_loop(0, group // together, some_heads, 0)

    def turn(step, carry):
        phase = step // 2
        other = lax.rem(step, 2)
        if square:
            off_a = phase
            off_b = jnp.where(phase == 1, 2, jnp.where(phase == 2, 1, phase))
        else:
            off_a = phase
            off_b = phase
        which = jnp.where(other == 0, core, 1 - core)
        slot_a = chip_at(off_a) * 2 + which
        slot_b = chip_at(off_b) * 2 + which

        @pl.when(step > 0)
        def _():
            kv_copy(slot_a, 0, partner, 0).wait_recv()
            kv_copy(slot_b, 1, partner, 0).wait_recv()

        if square:
            @pl.when(step == 2)
            def _():
                relay(0).start()
                relay(1).start()

        @pl.when((other == 0) & (step > 0))
        def _():
            to_partner(off_a, 0).start()
            to_partner(off_b, 1).start()

        attend(slot_a, slot_b)
        return carry

    lax.fori_loop(0, devices, turn, 0)

    live = low < high

    def finish(g, carry):
        whole = jnp.sum(total[g], axis=1, keepdims=True)
        result = jnp.where(live, numer[g] / jnp.where(live, whole, 1.0), 0.0)
        attended[:, pl.ds(pl.multiple_of(g * head_dim, head_dim), head_dim)] = result.astype(
            jnp.bfloat16
        )
        return carry

    lax.fori_loop(0, group, finish, 0)
    fetch.wait()

    piece = 512 if columns % 512 == 0 else columns
    chunk_rows = rows // chunks

    def project(dest):
        def block(j, carry):
            where = pl.ds(pl.multiple_of(dest * columns + j * piece, LANES), piece)
            term[:, where] = jnp.dot(
                attended[...], weight[:, where], preferred_element_type=jnp.float32
            )
            return carry

        lax.fori_loop(0, columns // piece, block, 0)

    def chunk_of(c):
        return pl.ds(pl.multiple_of(c * chunk_rows, chunk_rows), chunk_rows)

    def block_of(dest):
        return pl.ds(pl.multiple_of(dest * columns, LANES), columns)

    def right_copy(i, c):
        return pltpu.make_async_remote_copy(
            src_ref=sent.at[heads - 1 - i, chunk_of(c), :],
            dst_ref=from_left.at[i, chunk_of(c), :],
            send_sem=right_send.at[i, c],
            recv_sem=right_recv.at[i, c],
            device_id=(me, h + 1),
            device_id_type=MESH,
        )

    def left_copy(i, c):
        return pltpu.make_async_remote_copy(
            src_ref=sent.at[i, chunk_of(c), :],
            dst_ref=from_right.at[i, chunk_of(c), :],
            send_sem=left_send.at[i, c],
            recv_sem=left_recv.at[i, c],
            device_id=(me, h - 1),
            device_id_type=MESH,
        )

    def pass_on(dest, i, c, copy, arrived, first):
        @pl.when(first)
        def _():
            sent[dest, chunk_of(c), :] = term[chunk_of(c), block_of(dest)].astype(sent.dtype)

        @pl.when(jnp.logical_not(first))
        def _():
            copy(i, c).wait_recv()
            sent[dest, chunk_of(c), :] = (
                term[chunk_of(c), block_of(dest)]
                + arrived[i, chunk_of(c), :].astype(jnp.float32)
            ).astype(sent.dtype)

        copy(i, c).start()

    def spread(i, carry):
        far = heads - 1 - i

        @pl.when(h < far)
        def _():
            project(far)

        @pl.when(h > i)
        def _():
            project(i)

        def one_chunk(c, inner):
            @pl.when(h < far)
            def _():
                pass_on(far, i, c, right_copy, from_left, h == 0)

            @pl.when(h > i)
            def _():
                pass_on(i, i, c, left_copy, from_right, h == heads - 1)

            return inner

        lax.fori_loop(0, chunks, one_chunk, 0)
        return carry

    lax.fori_loop(0, heads - 1, spread, 0)
    project(h)

    def gather(c, carry):
        out_ref[chunk_of(c), :] = term[chunk_of(c), block_of(h)]

        @pl.when(h < heads - 1)
        def _():
            left_copy(h, c).wait_recv()
            out_ref[chunk_of(c), :] += from_right[h, chunk_of(c), :].astype(jnp.float32)

        @pl.when(h > 0)
        def _():
            right_copy(heads - 1 - h, c).wait_recv()
            out_ref[chunk_of(c), :] += from_left[heads - 1 - h, chunk_of(c), :].astype(jnp.float32)

        return carry

    lax.fori_loop(0, chunks, gather, 0)

    for offset in range(chips):
        for half in range(2):
            to_partner(offset, half).wait_send()
            if square and offset == 3:
                relay(half).wait_send()
            elif offset > 0:
                outgoing(offset, half).wait_send()

    def drain(i, carry):
        def one_chunk(c, inner):
            @pl.when(h < heads - 1 - i)
            def _():
                right_copy(i, c).wait_send()

            @pl.when(h > i)
            def _():
                left_copy(i, c).wait_send()

            return inner

        lax.fori_loop(0, chunks, one_chunk, 0)
        return carry

    lax.fori_loop(0, heads - 1, drain, 0)


def shards(
    queries, image_keys, image_values, layer_input, out_weight, tile_counts, image_range, attn_gate
):
    devices = lax.axis_size("seq")
    heads = lax.axis_size("head")
    rows, width = queries.shape
    tile_rows, head_dim = image_keys.shape
    group = width // head_dim
    columns = layer_input.shape[1]
    padded = round_up(tile_rows, LANES)
    send_rows = round_up(tile_rows, PACK)
    split = round_up(padded // 2, LANES)
    chunks = 4 if rows % (4 * PACK) == 0 else 1
    images = tile_counts.shape[0]
    kv = jnp.pad(jnp.stack([image_keys, image_values]), ((0, 0), (0, padded - tile_rows), (0, 0)))
    plan = (devices, heads, tile_rows, split, send_rows, images, chunks)
    low = jnp.bfloat16
    vmem = pl.BlockSpec(memory_space=pltpu.VMEM)
    hops = max(heads - 1, 1)
    summed = pl.pallas_call(
        functools.partial(kernel, plan),
        out_shape=jax.ShapeDtypeStruct((rows, columns), jnp.float32),
        in_specs=[
            pl.BlockSpec(memory_space=pltpu.SMEM),
            vmem,
            vmem,
            pl.BlockSpec(memory_space=pl.ANY),
            pl.BlockSpec(memory_space=pl.ANY),
        ],
        out_specs=vmem,
        scratch_shapes=[
            pltpu.VMEM((devices, 2, padded, head_dim), low),
            pltpu.VMEM(out_weight.shape, low),
            pltpu.VMEM((group, rows, 1), jnp.float32),
            pltpu.VMEM((group, rows, LANES), jnp.float32),
            pltpu.VMEM((group, rows, head_dim), jnp.float32),
            pltpu.VMEM((rows, width), low),
            pltpu.VMEM((rows, columns * heads), jnp.float32),
            pltpu.VMEM((heads, rows, columns), low),
            pltpu.VMEM((hops, rows, columns), low),
            pltpu.VMEM((hops, rows, columns), low),
            pltpu.SemaphoreType.DMA,
            pltpu.SemaphoreType.DMA,
            pltpu.SemaphoreType.DMA((devices, 2)),
            pltpu.SemaphoreType.DMA((devices, 2)),
            pltpu.SemaphoreType.DMA((hops, chunks)),
            pltpu.SemaphoreType.DMA((hops, chunks)),
            pltpu.SemaphoreType.DMA((hops, chunks)),
            pltpu.SemaphoreType.DMA((hops, chunks)),
        ],
        compiler_params=pltpu.CompilerParams(
            collective_id=0, has_side_effects=True, vmem_limit_bytes=62 * 1024 * 1024
        ),
    )(tile_counts, queries, image_range.T, kv, out_weight)
    gate = jnp.tanh(attn_gate[0])
    return (layer_input.astype(jnp.float32) + gate * summed).astype(jnp.bfloat16)


def solution(mesh):
    in_specs = (
        P("seq", "head"),
        P("seq", "head"),
        P("seq", "head"),
        P("seq", "head"),
        P("head", None),
        P(),
        P(None, "seq"),
        P(),
    )
    out_specs = P("seq", "head")
    return jax.shard_map(shards, mesh=mesh, in_specs=in_specs, out_specs=out_specs, check_vma=False)
```

profile of v0, /device:TPU:16, one launch (start us, length us, event | category | flops | bytes accessed | tf_op | source)
XLA Modules:
  0.0 129.5 jit_solution(2770775412209642450)
XLA Ops:
  0.0 2.2 %fusion.2.kv_hbm = bf16[2,1664,128]{2,1,0:T(8,128)(2,1)} fusion(bf16[1,1601,128]{2,1,0:T(8,128)(2,1)} %bitcast.4, bf16[1,1601,128]{2,1,0:T(8,128)(2,1)} %bitcast.5), kind=kLoop, calls=%fused_computation.4 | loop fusion | flops 2981888 | bytes 1671680 | tf_op jit(solution)/shard_map/stack | solution.py:402
  2.2 1.4 %copy.9 = s32[2,192]{0,1:T(8,128)} copy(s32[2,192]{1,0:T(2,128)} %param.14) | data formatting | bytes 3072 | tf_op args[6]
  3.6 0.0 copy-start
  3.6 122.7 %shard_map.82 = f32[192,2048]{1,0:T(8,128)} custom-call(s32[4]{0:T(128)} %counts_ref.1, bf16[192,1024]{1,0:T(8,128)(2,1)} %q_ref.1, s32[192,2]{1,0:T(8,128)} %bitcast.6, bf16[2,1664,128]{2,1,0:T(8,128)(2,1)} %fusion.2.kv_hbm, bf16[1024,8192]{1,0:T(8,128)(2,1)} %w_hbm.1), custom_call_target="tpu_custom_call" | custom-call | tf_op jit(solution)/shard_map/pallas_call | solution.py:407
  127.0 0.0 copy-done
  127.0 2.5 %add_convert_fusion = bf16[192,2048]{1,0:T(8,128)(2,1)} fusion(f32[192,2048]{1,0:T(8,128)} %shard_map.82, bf16[192,2048]{1,0:T(8,128)(2,1)S(1)} %copy-done, f32[]{:T(128)} %bitcast), kind=kLoop, calls=%fused_computation.3 | loop fusion | flops 1572864 | bytes 3145732 | tf_op jit(solution)/shard_map/convert_element_type | solution.py:443
Async XLA Ops:
  3.6 123.4 %copy-start = (bf16[192,2048]{1,0:T(8,128)(2,1)S(1)}, bf16[192,2048]{1,0:T(8,128)(2,1)}, u32[]{:S(2)}) copy-start(bf16[192,2048]{1,0:T(8,128)(2,1)} %param.11) | copy-start | bytes 2359300
where the time goes:
time: 130 us; the launch traced here: 129 us
  Pallas kernels  123 us (95%)
  other arithmetic  4.67 us (4%)
  local copies, waits for them, and re-layouts  1.45 us (1%)
    pallas_call x1, Pallas kernels, shards(): pl.pallas_call(functools.partial(kernel, plan), out_shape=jax.ShapeDtypeS...  123 us

commit v1 on v0

--- a/solution.py
+++ b/solution.py
@@ -22,16 +22,25 @@
 def kernel(
     plan,
     counts_ref,
+    gate_ref,
     q_ref,
     range_ref,
-    kv_hbm,
+    k_hbm,
+    v_hbm,
     w_hbm,
+    x_hbm,
     out_ref,
     kv,
+    staged,
     weight,
+    residual,
+    q_wide,
+    bounds,
+    scores,
+    values,
     run_max,
-    total,
     numer,
+    turned,
     attended,
     term,
     sent,
@@ -39,6 +48,7 @@
     from_right,
     own_sem,
     weight_sem,
+    residual_sem,
     kv_send,
     kv_recv,
     right_send,
@@ -46,7 +56,7 @@
     left_send,
     left_recv,
 ):
-    devices, heads, tile_rows, split, send_rows, images, chunks = plan
+    devices, heads, tile_rows, split, padded, images, chunks, strip = plan
     square = devices == 8
     chips = devices // 2
     me = lax.axis_index("seq")
@@ -57,9 +67,9 @@
     rows, width = q_ref.shape
     head_dim = kv.shape[3]
     group = width // head_dim
-    padded = kv.shape[2]
+    strips = group * rows // strip
     columns = out_ref.shape[1]
-    halves = ((0, split), (split, send_rows - split))
+    halves = ((0, split), (split, padded - split))
 
     def chip_at(offset):
         if square:
@@ -71,12 +81,18 @@
     def at(target):
         return (target, h)
 
-    own = pltpu.make_async_copy(
-        kv_hbm.at[:, pl.ds(0, send_rows), :], kv.at[me, :, pl.ds(0, send_rows), :], own_sem
-    )
-    own.start()
+    own = [
+        pltpu.make_async_copy(
+            source, staged.at[which], own_sem.at[which]
+        )
+        for which, source in enumerate((k_hbm, v_hbm))
+    ]
+    for copy in own:
+        copy.start()
     fetch = pltpu.make_async_copy(w_hbm, weight, weight_sem)
     fetch.start()
+    take = pltpu.make_async_copy(x_hbm, residual, residual_sem)
+    take.start()
 
     barrier = pltpu.get_barrier_semaphore()
     pl.semaphore_signal(barrier, inc=1, device_id=at(partner), device_id_type=MESH)
@@ -98,15 +114,27 @@
 
     ends = jnp.where(h > 0, 1, 0) + jnp.where(h < heads - 1, 1, 0)
 
+    factor = math.log2(math.e) / math.sqrt(head_dim)
     run_max[...] = jnp.full_like(run_max, NEG)
-    total[...] = jnp.zeros_like(total)
     numer[...] = jnp.zeros_like(numer)
-    if send_rows < padded:
-        kv[:, :, send_rows:, :] = jnp.zeros(
-            (devices, 2, padded - send_rows, head_dim), kv.dtype
-        )
+    values[...] = jnp.ones_like(values)
+    for g in range(group):
+        exact = q_ref[:, g * head_dim : (g + 1) * head_dim].astype(jnp.float32) * factor
+        high = exact.astype(jnp.bfloat16)
+        part = pl.ds(g * rows, rows)
+        q_wide[:head_dim, part] = high.T
+        q_wide[head_dim:, part] = (exact - high.astype(jnp.float32)).astype(jnp.bfloat16).T
+        bounds[:, part] = range_ref[...]
+    whole_rows = tile_rows // PACK * PACK
+    for which, copy in enumerate(own):
+        copy.wait()
+        kv[me, which, :whole_rows, :] = staged[which, :whole_rows, :]
+        if whole_rows < padded:
+            rest = staged[which, whole_rows:, :]
+            kv[me, which, whole_rows:, :] = jnp.concatenate(
+                [rest, jnp.zeros((padded - tile_rows, head_dim), rest.dtype)], axis=0
+            )
     pl.semaphore_wait(barrier, greeted + ends)
-    own.wait()
 
     def kv_copy(slot, half, target, lane):
         start, size = halves[half]
@@ -152,66 +180,58 @@
             image = image + jnp.where(end <= slot, 1, 0)
         return image
 
-    low = range_ref[:, 0:1]
-    high = range_ref[:, 1:2]
-    factor = math.log2(math.e) / math.sqrt(head_dim)
-    last = padded - LANES
-    real = tile_rows - last
-
-    def lane_tiles(value):
-        return [value[:, j : j + LANES] for j in range(0, value.shape[1], LANES)]
+    real = tile_rows - split
+    edge = real // PACK * PACK
 
     def attend(slot_a, slot_b):
         image_a, image_b = image_of(slot_a), image_of(slot_b)
-        ok_a = (low <= image_a) & (image_a < high)
-        ok_b = (low <= image_b) & (image_b < high)
-
-        def one_head(g):
-            q = q_ref[:, pl.ds(pl.multiple_of(g * head_dim, head_dim), head_dim)]
-            contract = (((1,), (1,)), ((), ()))
-            s_a = lax.dot_general(
-                q, kv[slot_a, 0, :split, :], contract, preferred_element_type=jnp.float32
-            )
-            s_b = lax.dot_general(
-                q, kv[slot_b, 0, split:, :], contract, preferred_element_type=jnp.float32
-            )
-            edge = s_b[:, last - split :]
-            lane = lax.broadcasted_iota(jnp.int32, edge.shape, 1)
-            s_b = jnp.concatenate(
-                [s_b[:, : last - split], jnp.where(lane < real, edge, NEG)], axis=1
-            )
-            top_a = jnp.max(functools.reduce(jnp.maximum, lane_tiles(s_a)), axis=1, keepdims=True)
-            top_b = jnp.max(functools.reduce(jnp.maximum, lane_tiles(s_b)), axis=1, keepdims=True)
+        values[:head_dim, :split] = kv[slot_a, 1, :split, :].T
+        values[:head_dim, split:] = kv[slot_b, 1, split:, :].T
+
+        def lanes(g):
+            return slice(g * strip, (g + 1) * strip)
+
+        def allowed(g, image):
+            low, high = bounds[0:1, lanes(g)], bounds[1:2, lanes(g)]
+            return (low <= image) & (image < high)
+
+        def score(g):
+            q = q_wide[:, lanes(g)]
+
+            def one(keys):
+                return jnp.dot(
+                    jnp.concatenate([keys, keys], axis=1), q, preferred_element_type=jnp.float32
+                )
+
+            s_a = one(kv[slot_a, 0, :split, :])
+            s_b = one(kv[slot_b, 0, split:, :])
+            row = lax.broadcasted_iota(jnp.int32, s_b[edge:].shape, 0)
+            s_b = jnp.concatenate([s_b[:edge], jnp.where(row < real - edge, s_b[edge:], NEG)], axis=0)
+            scores[g % 2, :split, :] = s_a
+            scores[g % 2, split:, :] = s_b
+            return jnp.max(s_a, axis=0, keepdims=True), jnp.max(s_b, axis=0, keepdims=True)
+
+        def mix(g, tops):
+            ok_a, ok_b = allowed(g, image_a), allowed(g, image_b)
             old = run_max[g]
             new = jnp.maximum(
-                old, jnp.maximum(jnp.where(ok_a, top_a, NEG), jnp.where(ok_b, top_b, NEG))
+                old, jnp.maximum(jnp.where(ok_a, tops[0], NEG), jnp.where(ok_b, tops[1], NEG))
             )
-            base_a = jnp.where(ok_a, new, BIG) * factor
-            base_b = jnp.where(ok_b, new, BIG) * factor
-            p_a = jnp.exp2(s_a * factor - base_a)
-            p_b = jnp.exp2(s_b * factor - base_b)
-            alpha = jnp.exp2((old - new) * factor)
+            base_a = jnp.where(ok_a, new, BIG)
+            base_b = jnp.where(ok_b, new, BIG)
+            p_a = jnp.exp2(scores[g % 2, :split, :] - base_a).astype(jnp.bfloat16)
+            p_b = jnp.exp2(scores[g % 2, split:, :] - base_b).astype(jnp.bfloat16)
             run_max[g] = new
-            total[g] = total[g] * alpha + functools.reduce(
-                jnp.add, lane_tiles(p_a) + lane_tiles(p_b)
+            mixed = jnp.dot(
+                values[...], jnp.concatenate([p_a, p_b], axis=0), preferred_element_type=jnp.float32
             )
-            mixed = jnp.dot(
-                p_a.astype(jnp.bfloat16), kv[slot_a, 1, :split, :],
-                preferred_element_type=jnp.float32,
-            ) + jnp.dot(
-                p_b.astype(jnp.bfloat16), kv[slot_b, 1, split:, :],
-                preferred_element_type=jnp.float32,
-            )
-            numer[g] = numer[g] * alpha + mixed
-
-        together = math.gcd(group, 4)
-
-        def some_heads(block, carry):
-            for k in range(together):
-                one_head(block * together + k)
-            return carry
-
-        lax.fori_loop(0, group // together, some_heads, 0)
+            numer[g] = numer[g] * jnp.exp2(old - new) + mixed
+
+        tops = score(0)
+        for g in range(strips):
+            later = score(g + 1) if g + 1 < strips else None
+            mix(g, tops)
+            tops = later
 
     def turn(step, carry):
         phase = step // 2
@@ -247,17 +267,16 @@
 
     lax.fori_loop(0, devices, turn, 0)
 
-    live = low < high
-
-    def finish(g, carry):
-        whole = jnp.sum(total[g], axis=1, keepdims=True)
-        result = jnp.where(live, numer[g] / jnp.where(live, whole, 1.0), 0.0)
-        attended[:, pl.ds(pl.multiple_of(g * head_dim, head_dim), head_dim)] = result.astype(
-            jnp.bfloat16
-        )
-        return carry
-
-    lax.fori_loop(0, group, finish, 0)
+    for g in range(strips):
+        part = slice(g * strip, (g + 1) * strip)
+        live = bounds[0:1, part] < bounds[1:2, part]
+        whole = numer[g, head_dim : head_dim + 1, :]
+        result = jnp.where(live, numer[g, :head_dim, :] / jnp.where(live, whole, 1.0), 0.0)
+        turned[part, :] = result.T
+    for g in range(group):
+        attended[:, g * head_dim : (g + 1) * head_dim] = turned[
+            g * rows : (g + 1) * rows, :
+        ].astype(jnp.bfloat16)
     fetch.wait()
 
     piece = 512 if columns % 512 == 0 else columns
@@ -342,19 +361,25 @@
     lax.fori_loop(0, heads - 1, spread, 0)
     project(h)
 
+    take.wait()
+    gate = jnp.tanh(jnp.full((8, LANES), gate_ref[0], jnp.float32))[0:1, 0:1]
+
     def gather(c, carry):
-        out_ref[chunk_of(c), :] = term[chunk_of(c), block_of(h)]
-
         @pl.when(h < heads - 1)
         def _():
             left_copy(h, c).wait_recv()
-            out_ref[chunk_of(c), :] += from_right[h, chunk_of(c), :].astype(jnp.float32)
+            term[chunk_of(c), block_of(h)] += from_right[h, chunk_of(c), :].astype(jnp.float32)
 
         @pl.when(h > 0)
         def _():
             right_copy(heads - 1 - h, c).wait_recv()
-            out_ref[chunk_of(c), :] += from_left[heads - 1 - h, chunk_of(c), :].astype(jnp.float32)
-
+            term[chunk_of(c), block_of(h)] += from_left[heads - 1 - h, chunk_of(c), :].astype(
+                jnp.float32
+            )
+
+        out_ref[chunk_of(c), :] = (
+            residual[chunk_of(c), :].astype(jnp.float32) + gate * term[chunk_of(c), block_of(h)]
+        ).astype(out_ref.dtype)
         return carry
 
     lax.fori_loop(0, chunks, gather, 0)
@@ -394,38 +419,41 @@
     tile_rows, head_dim = image_keys.shape
     group = width // head_dim
     columns = layer_input.shape[1]
-    padded = round_up(tile_rows, LANES)
-    send_rows = round_up(tile_rows, PACK)
-    split = round_up(padded // 2, LANES)
+    padded = round_up(tile_rows, PACK)
+    split = max(round_up(padded // 2 - LANES, LANES), LANES)
     chunks = 4 if rows % (4 * PACK) == 0 else 1
     images = tile_counts.shape[0]
-    kv = jnp.pad(jnp.stack([image_keys, image_values]), ((0, 0), (0, padded - tile_rows), (0, 0)))
-    plan = (devices, heads, tile_rows, split, send_rows, images, chunks)
+    strip = math.gcd(group * rows, 2 * LANES)
+    strips = group * rows // strip
+    plan = (devices, heads, tile_rows, split, padded, images, chunks, strip)
     low = jnp.bfloat16
     vmem = pl.BlockSpec(memory_space=pltpu.VMEM)
+    smem = pl.BlockSpec(memory_space=pltpu.SMEM)
+    hbm = pl.BlockSpec(memory_space=pl.ANY)
     hops = max(heads - 1, 1)
-    summed = pl.pallas_call(
+    return pl.pallas_call(
         functools.partial(kernel, plan),
-        out_shape=jax.ShapeDtypeStruct((rows, columns), jnp.float32),
-        in_specs=[
-            pl.BlockSpec(memory_space=pltpu.SMEM),
-            vmem,
-            vmem,
-            pl.BlockSpec(memory_space=pl.ANY),
-            pl.BlockSpec(memory_space=pl.ANY),
-        ],
+        out_shape=jax.ShapeDtypeStruct((rows, columns), low),
+        in_specs=[smem, smem, vmem, vmem, hbm, hbm, hbm, hbm],
         out_specs=vmem,
         scratch_shapes=[
             pltpu.VMEM((devices, 2, padded, head_dim), low),
+            pltpu.VMEM((2, tile_rows, head_dim), low),
             pltpu.VMEM(out_weight.shape, low),
-            pltpu.VMEM((group, rows, 1), jnp.float32),
-            pltpu.VMEM((group, rows, LANES), jnp.float32),
-            pltpu.VMEM((group, rows, head_dim), jnp.float32),
+            pltpu.VMEM((rows, columns), low),
+            pltpu.VMEM((2 * head_dim, group * rows), low),
+            pltpu.VMEM((2, group * rows), jnp.int32),
+            pltpu.VMEM((2, padded, strip), jnp.float32),
+            pltpu.VMEM((head_dim + PACK, padded), low),
+            pltpu.VMEM((strips, 1, strip), jnp.float32),
+            pltpu.VMEM((strips, head_dim + PACK, strip), jnp.float32),
+            pltpu.VMEM((group * rows, head_dim), jnp.float32),
             pltpu.VMEM((rows, width), low),
             pltpu.VMEM((rows, columns * heads), jnp.float32),
             pltpu.VMEM((heads, rows, columns), low),
             pltpu.VMEM((hops, rows, columns), low),
             pltpu.VMEM((hops, rows, columns), low),
+            pltpu.SemaphoreType.DMA((2,)),
             pltpu.SemaphoreType.DMA,
             pltpu.SemaphoreType.DMA,
             pltpu.SemaphoreType.DMA((devices, 2)),
@@ -438,9 +466,10 @@
         compiler_params=pltpu.CompilerParams(
             collective_id=0, has_side_effects=True, vmem_limit_bytes=62 * 1024 * 1024
         ),
-    )(tile_counts, queries, image_range.T, kv, out_weight)
-    gate = jnp.tanh(attn_gate[0])
-    return (layer_input.astype(jnp.float32) + gate * summed).astype(jnp.bfloat16)
+    )(
+        tile_counts, attn_gate, queries, image_range, image_keys, image_values, out_weight,
+        layer_input,
+    )
 
 
 def solution(mesh):

time: 130 us -> 104 us (0.80)
  Pallas kernels: 123 us -> 101 us
  other arithmetic: 4.67 us -> 0 us
    pallas_call x1, Pallas kernels: 123 us -> 101 us  [shards(): pl.pallas_call(functools.partial(kernel, plan), out_shape=jax.ShapeDtypeS...]
    convert_element_type x1 -> x0, other arithmetic: 2.5 us -> none  [shards(): (layer_input.astype(jnp.float32) + gate * summed).astype(jnp.bfloat16)]
    another operation x1 -> x0, other arithmetic: 2.17 us -> none  [shards(): jnp.stack([image_keys, image_values])]
where the time goes in v1:
time: 104 us
  Pallas kernels  101 us (97%)
  local copies, waits for them, and re-layouts  2.09 us (2%)
    pallas_call x1, Pallas kernels, shards(): pl.pallas_call(functools.partial(kernel, plan), out_shape=jax.ShapeDtypeS...  101 us
    unnamed x1, local copies, waits for them, and re-layouts  2.09 us

profile of v1, /device:TPU:16, one launch (start us, length us, event | category | flops | bytes accessed | tf_op | source)
XLA Modules:
  0.0 104.2 jit_solution(6954261319070840266)
XLA Ops:
  0.7 101.5 %shard_map.82 = bf16[192,2048]{1,0:T(8,128)(2,1)} custom-call(s32[4]{0:T(128)} %counts_ref.1, f32[1]{0:T(128)S(6)} %copy.10.gate_ref, bf16[192,1024]{1,0:T(8,128)(2,1)} %q_ref.1, s32[2,192]{1,0:T(2,128)} %range_ref.1, bf16[1601,128]{1,0:T(8,128)(2,1)} %k_hbm.1, bf16[1601,128]{1,0:T(8,128)(2,1)} %v_hbm.1, bf16[1024,8192]{1,0:T(8,128)(2,1)} %w_hbm.1, ...), custom_call_target="tpu_custom_call" | custom-call | tf_op jit(solution)/shard_map/pallas_call | solution.py:434
  102.1 2.1 %copy.11 = bf16[192,2048]{1,0:T(8,128)(2,1)} copy(bf16[192,2048]{1,0:T(8,128)(2,1)} %shard_map.82) | data formatting | bytes 1572864

commit v2 on v1

--- a/solution.py
+++ b/solution.py
@@ -13,6 +13,7 @@
 BIG = 1e30
 LANES = 128
 PACK = 16
+LAG = 1
 
 
 def round_up(value, unit):
@@ -55,6 +56,12 @@
     right_recv,
     left_send,
     left_recv,
+    lent_weight,
+    lent_rows,
+    lent_send,
+    lent_recv,
+    rows_send,
+    rows_recv,
 ):
     devices, heads, tile_rows, split, padded, images, chunks, strip = plan
     square = devices == 8
@@ -97,12 +104,10 @@
     barrier = pltpu.get_barrier_semaphore()
     pl.semaphore_signal(barrier, inc=1, device_id=at(partner), device_id_type=MESH)
     for offset in range(1, chips):
-        if square and offset == 3:
-            continue
         pl.semaphore_signal(
             barrier, inc=1, device_id=at(chip_at(offset) * 2 + core), device_id_type=MESH
         )
-    greeted = 1 + (2 if square else chips - 1)
+    greeted = chips
 
     @pl.when(h > 0)
     def _():
@@ -160,6 +165,46 @@
             chip_at(source) * 2 + core, half, chip_at(3 - source) * 2 + core, chips + 3
         )
 
+    share = width // devices
+    lends = (h == 0) | (h == heads - 1)
+    borrows = (h == 1) | (h == heads - 2)
+    borrower = jnp.where(h < 2, 1, heads - 2)
+
+    def lent_piece(slot):
+        return lent_weight.at[pl.ds(pl.multiple_of(slot * share, share), share), :]
+
+    lend = pltpu.make_async_remote_copy(
+        src_ref=w_hbm.at[
+            pl.ds(pl.multiple_of(me * share, share), share),
+            pl.ds(pl.multiple_of(borrower * columns, LANES), columns),
+        ],
+        dst_ref=lent_piece(me),
+        send_sem=lent_send.at[0],
+        recv_sem=lent_recv.at[me],
+        device_id=(me, borrower),
+        device_id_type=MESH,
+    )
+
+    @pl.when(lends)
+    def _():
+        lend.start()
+
+    def lent_copy(slot, target, lane):
+        return pltpu.make_async_remote_copy(
+            src_ref=lent_piece(slot),
+            dst_ref=lent_piece(slot),
+            send_sem=lent_send.at[lane],
+            recv_sem=lent_recv.at[slot],
+            device_id=at(target),
+            device_id_type=MESH,
+        )
+
+    def lent_out(offset):
+        return lent_copy(me, chip_at(offset) * 2 + core, chips + offset)
+
+    def lent_over(offset):
+        return lent_copy(chip_at(offset) * 2 + core, partner, 1 + offset)
+
     if square:
         outgoing(1, 0).start()
         outgoing(2, 1).start()
@@ -279,6 +324,22 @@
         ].astype(jnp.bfloat16)
     fetch.wait()
 
+    @pl.when(borrows)
+    def _():
+        lend.wait_recv()
+        for offset in range(1, chips):
+            lent_out(offset).start()
+        lent_over(0).start()
+
+    lend_rows = pltpu.make_async_remote_copy(
+        src_ref=attended,
+        dst_ref=lent_rows,
+        send_sem=rows_send,
+        recv_sem=rows_recv,
+        device_id=(me, borrower),
+        device_id_type=MESH,
+    )
+
     piece = 512 if columns % 512 == 0 else columns
     chunk_rows = rows // chunks
 
@@ -333,44 +394,74 @@
 
         copy(i, c).start()
 
-    def spread(i, carry):
-        far = heads - 1 - i
-
-        @pl.when(h < far)
-        def _():
-            project(far)
-
-        @pl.when(h > i)
-        def _():
-            project(i)
-
-        def one_chunk(c, inner):
-            @pl.when(h < far)
+    def spread(t, carry):
+        to_right = t - LAG * h
+        to_left = t - LAG * (heads - 1 - h)
+
+        @pl.when(borrows & (t == (heads - 3) * chunks + LAG))
+        def _():
+            for offset in range(1, chips):
+                lent_copy(chip_at(offset) * 2 + core, partner, 0).wait_recv()
+                lent_over(offset).start()
+
+        @pl.when((to_right >= 0) & (to_right < jnp.minimum(heads - 1 - h, heads - 2) * chunks))
+        def _():
+            i = to_right // chunks
+            c = lax.rem(to_right, chunks)
+
+            @pl.when(c == 0)
             def _():
-                pass_on(far, i, c, right_copy, from_left, h == 0)
-
-            @pl.when(h > i)
+                project(heads - 1 - i)
+
+            pass_on(heads - 1 - i, i, c, right_copy, from_left, h == 0)
+
+        @pl.when((to_left >= 0) & (to_left < jnp.minimum(h, heads - 2) * chunks))
+        def _():
+            i = to_left // chunks
+            c = lax.rem(to_left, chunks)
+
+            @pl.when(c == 0)
             def _():
-                pass_on(i, i, c, left_copy, from_right, h == heads - 1)
-
-            return inner
-
-        lax.fori_loop(0, chunks, one_chunk, 0)
+                project(i)
+
+            pass_on(i, i, c, left_copy, from_right, h == heads - 1)
+
         return carry
 
-    lax.fori_loop(0, heads - 1, spread, 0)
+    lax.fori_loop(0, (heads - 2) * chunks + LAG * (heads - 1), spread, 0)
+
+    @pl.when(lends)
+    def _():
+        lend_rows.start()
+
     project(h)
+
+    @pl.when(borrows)
+    def _():
+        for offset in range(chips):
+            lent_copy(chip_at(offset) * 2 + 1 - core, partner, 0).wait_recv()
+        lend_rows.wait_recv()
+
+        def block(j, carry):
+            where = pl.ds(pl.multiple_of(j * piece, LANES), piece)
+            into = pl.ds(pl.multiple_of(h * columns + j * piece, LANES), piece)
+            term[:, into] += jnp.dot(
+                lent_rows[...], lent_weight[:, where], preferred_element_type=jnp.float32
+            )
+            return carry
+
+        lax.fori_loop(0, columns // piece, block, 0)
 
     take.wait()
     gate = jnp.tanh(jnp.full((8, LANES), gate_ref[0], jnp.float32))[0:1, 0:1]
 
     def gather(c, carry):
-        @pl.when(h < heads - 1)
+        @pl.when((h < heads - 1) & (h != heads - 2))
         def _():
             left_copy(h, c).wait_recv()
             term[chunk_of(c), block_of(h)] += from_right[h, chunk_of(c), :].astype(jnp.float32)
 
-        @pl.when(h > 0)
+        @pl.when((h > 0) & (h != 1))
         def _():
             right_copy(heads - 1 - h, c).wait_recv()
             term[chunk_of(c), block_of(h)] += from_left[heads - 1 - h, chunk_of(c), :].astype(
@@ -407,7 +498,19 @@
         lax.fori_loop(0, chunks, one_chunk, 0)
         return carry
 
-    lax.fori_loop(0, heads - 1, drain, 0)
+    lax.fori_loop(0, heads - 2, drain, 0)
+
+    @pl.when(lends)
+    def _():
+        lend.wait_send()
+        lend_rows.wait_send()
+
+    @pl.when(borrows)
+    def _():
+        for offset in range(chips):
+            lent_over(offset).wait_send()
+            if offset > 0:
+                lent_out(offset).wait_send()
 
 
 def shards(
@@ -430,7 +533,7 @@
     vmem = pl.BlockSpec(memory_space=pltpu.VMEM)
     smem = pl.BlockSpec(memory_space=pltpu.SMEM)
     hbm = pl.BlockSpec(memory_space=pl.ANY)
-    hops = max(heads - 1, 1)
+    hops = heads - 2
     return pl.pallas_call(
         functools.partial(kernel, plan),
         out_shape=jax.ShapeDtypeStruct((rows, columns), low),
@@ -462,6 +565,12 @@
             pltpu.SemaphoreType.DMA((hops, chunks)),
             pltpu.SemaphoreType.DMA((hops, chunks)),
             pltpu.SemaphoreType.DMA((hops, chunks)),
+            pltpu.VMEM((width, columns), low),
+            pltpu.VMEM((rows, width), low),
+            pltpu.SemaphoreType.DMA((devices + 1,)),
+            pltpu.SemaphoreType.DMA((devices,)),
+            pltpu.SemaphoreType.DMA,
+            pltpu.SemaphoreType.DMA,
         ],
         compiler_params=pltpu.CompilerParams(
             collective_id=0, has_side_effects=True, vmem_limit_bytes=62 * 1024 * 1024

time: 104 us -> 91 us (0.88)
  Pallas kernels: 101 us -> 87.9 us
    pallas_call x1, Pallas kernels: 101 us -> 87.9 us  [shards(): pl.pallas_call(functools.partial(kernel, plan), out_shape=jax.ShapeDtypeS...]
where the time goes in v2:
time: 91 us; the launch traced here: 90.6 us
  Pallas kernels  87.9 us (97%)
  local copies, waits for them, and re-layouts  2.09 us (2%)
    pallas_call x1, Pallas kernels, shards(): pl.pallas_call(functools.partial(kernel, plan), out_shape=jax.ShapeDtypeS...  87.9 us
    unnamed x1, local copies, waits for them, and re-layouts  2.09 us

profile of v2, /device:TPU:16, one launch (start us, length us, event | category | flops | bytes accessed | tf_op | source)
XLA Modules:
  0.0 90.6 jit_solution(10342631026385136998)
XLA Ops:
  0.7 87.9 %shard_map.82 = bf16[192,2048]{1,0:T(8,128)(2,1)} custom-call(s32[4]{0:T(128)} %counts_ref.1, f32[1]{0:T(128)S(6)} %copy.10.gate_ref, bf16[192,1024]{1,0:T(8,128)(2,1)} %q_ref.1, s32[2,192]{1,0:T(2,128)} %range_ref.1, bf16[1601,128]{1,0:T(8,128)(2,1)} %k_hbm.1, bf16[1601,128]{1,0:T(8,128)(2,1)} %v_hbm.1, bf16[1024,8192]{1,0:T(8,128)(2,1)} %w_hbm.1, ...), custom_call_target="tpu_custom_call" | custom-call | tf_op jit(solution)/shard_map/pallas_call | solution.py:537
  88.5 2.1 %copy.11 = bf16[192,2048]{1,0:T(8,128)(2,1)} copy(bf16[192,2048]{1,0:T(8,128)(2,1)} %shard_map.82) | data formatting | bytes 1572864

commit v3 on v2

--- a/solution.py
+++ b/solution.py
@@ -119,6 +119,94 @@
 
     ends = jnp.where(h > 0, 1, 0) + jnp.where(h < heads - 1, 1, 0)
 
+    whole_rows = tile_rows // PACK * PACK
+    for which, copy in enumerate(own):
+        copy.wait()
+        kv[me, which, :whole_rows, :] = staged[which, :whole_rows, :]
+        if whole_rows < padded:
+            rest = staged[which, whole_rows:, :]
+            kv[me, which, whole_rows:, :] = jnp.concatenate(
+                [rest, jnp.zeros((padded - tile_rows, head_dim), rest.dtype)], axis=0
+            )
+    pl.semaphore_wait(barrier, greeted + ends)
+
+    def kv_copy(slot, half, target, lane):
+        start, size = halves[half]
+        piece = kv.at[slot, :, pl.ds(start, size), :]
+        return pltpu.make_async_remote_copy(
+            src_ref=piece,
+            dst_ref=piece,
+            send_sem=kv_send.at[lane, half],
+            recv_sem=kv_recv.at[slot, half],
+            device_id=at(target),
+            device_id_type=MESH,
+        )
+
+    def outgoing(offset, half):
+        return kv_copy(me, half, chip_at(offset) * 2 + core, chips + offset)
+
+    def to_partner(offset, half):
+        return kv_copy(chip_at(offset) * 2 + core, half, partner, offset)
+
+    def relay(half):
+        source = 1 if half == 0 else 2
+        return kv_copy(
+            chip_at(source) * 2 + core, half, chip_at(3 - source) * 2 + core, chips + 3
+        )
+
+    share = width // devices
+    lends = (h == 0) | (h == heads - 1)
+    borrows = (h == 1) | (h == heads - 2)
+    borrower = jnp.where(h < 2, 1, heads - 2)
+
+    def lent_piece(slot):
+        return lent_weight.at[pl.ds(pl.multiple_of(slot * share, share), share), :]
+
+    lend = pltpu.make_async_remote_copy(
+        src_ref=w_hbm.at[
+            pl.ds(pl.multiple_of(me * share, share), share),
+            pl.ds(pl.multiple_of(borrower * columns, LANES), columns),
+        ],
+        dst_ref=lent_piece(me),
+        send_sem=lent_send.at[0],
+        recv_sem=lent_recv.at[me],
+        device_id=(me, borrower),
+        device_id_type=MESH,
+    )
+
+    @pl.when(lends)
+    def _():
+        lend.start()
+
+    def lent_copy(slot, target, lane):
+        return pltpu.make_async_remote_copy(
+            src_ref=lent_piece(slot),
+            dst_ref=lent_piece(slot),
+            send_sem=lent_send.at[lane],
+            recv_sem=lent_recv.at[slot],
+            device_id=at(target),
+            device_id_type=MESH,
+        )
+
+    def lent_out(offset):
+        return lent_copy(me, chip_at(offset) * 2 + core, chips + offset)
+
+    def lent_over(offset):
+        return lent_copy(chip_at(offset) * 2 + core, partner, 1 + offset)
+
+    if square:
+        outgoing(1, 0).start()
+        outgoing(2, 1).start()
+        outgoing(1, 1).start()
+        outgoing(2, 0).start()
+    else:
+        for offset in range(1, chips):
+            for half in range(2):
+                outgoing(offset, half).start()
+
+    to_partner(0, 0).start()
+    to_partner(0, 1).start()
+
     factor = math.log2(math.e) / math.sqrt(head_dim)
     run_max[...] = jnp.full_like(run_max, NEG)
     numer[...] = jnp.zeros_like(numer)
@@ -130,93 +218,6 @@
         q_wide[:head_dim, part] = high.T
         q_wide[head_dim:, part] = (exact - high.astype(jnp.float32)).astype(jnp.bfloat16).T
         bounds[:, part] = range_ref[...]
-    whole_rows = tile_rows // PACK * PACK
-    for which, copy in enumerate(own):
-        copy.wait()
-        kv[me, which, :whole_rows, :] = staged[which, :whole_rows, :]
-        if whole_rows < padded:
-            rest = staged[which, whole_rows:, :]
-            kv[me, which, whole_rows:, :] = jnp.concatenate(
-                [rest, jnp.zeros((padded - tile_rows, head_dim), rest.dtype)], axis=0
-            )
-    pl.semaphore_wait(barrier, greeted + ends)
-
-    def kv_copy(slot, half, target, lane):
-        start, size = halves[half]
-        piece = kv.at[slot, :, pl.ds(start, size), :]
-        return pltpu.make_async_remote_copy(
-            src_ref=piece,
-            dst_ref=piece,
-            send_sem=kv_send.at[lane, half],
-            recv_sem=kv_recv.at[slot, half],
-            device_id=at(target),
-            device_id_type=MESH,
-        )
-
-    def outgoing(offset, half):
-        return kv_copy(me, half, chip_at(offset) * 2 + core, chips + offset)
-
-    def to_partner(offset, half):
-        return kv_copy(chip_at(offset) * 2 + core, half, partner, offset)
-
-    def relay(half):
-        source = 1 if half == 0 else 2
-        return kv_copy(
-            chip_at(source) * 2 + core, half, chip_at(3 - source) * 2 + core, chips + 3
-        )
-
-    share = width // devices
-    lends = (h == 0) | (h == heads - 1)
-    borrows = (h == 1) | (h == heads - 2)
-    borrower = jnp.where(h < 2, 1, heads - 2)
-
-    def lent_piece(slot):
-        return lent_weight.at[pl.ds(pl.multiple_of(slot * share, share), share), :]
-
-    lend = pltpu.make_async_remote_copy(
-        src_ref=w_hbm.at[
-            pl.ds(pl.multiple_of(me * share, share), share),
-            pl.ds(pl.multiple_of(borrower * columns, LANES), columns),
-        ],
-        dst_ref=lent_piece(me),
-        send_sem=lent_send.at[0],
-        recv_sem=lent_recv.at[me],
-        device_id=(me, borrower),
-        device_id_type=MESH,
-    )
-
-    @pl.when(lends)
-    def _():
-        lend.start()
-
-    def lent_copy(slot, target, lane):
-        return pltpu.make_async_remote_copy(
-            src_ref=lent_piece(slot),
-            dst_ref=lent_piece(slot),
-            send_sem=lent_send.at[lane],
-            recv_sem=lent_recv.at[slot],
-            device_id=at(target),
-            device_id_type=MESH,
-        )
-
-    def lent_out(offset):
-        return lent_copy(me, chip_at(offset) * 2 + core, chips + offset)
-
-    def lent_over(offset):
-        return lent_copy(chip_at(offset) * 2 + core, partner, 1 + offset)
-
-    if square:
-        outgoing(1, 0).start()
-        outgoing(2, 1).start()
-        outgoing(1, 1).start()
-        outgoing(2, 0).start()
-    else:
-        for offset in range(1, chips):
-            for half in range(2):
-                outgoing(offset, half).start()
-
-    to_partner(0, 0).start()
-    to_partner(0, 1).start()
 
     def image_of(slot):
         image, end = 0, 0

time: 91 us -> 91 us (level)
  no operation moved by 1% of the time
where the time goes in v3:
time: 91 us; the launch traced here: 90.6 us
  Pallas kernels  87.9 us (97%)
  local copies, waits for them, and re-layouts  2.09 us (2%)
    pallas_call x1, Pallas kernels, shards(): pl.pallas_call(functools.partial(kernel, plan), out_shape=jax.ShapeDtypeS...  87.9 us
    unnamed x1, local copies, waits for them, and re-layouts  2.09 us

profile of v3, /device:TPU:16, one launch (start us, length us, event | category | flops | bytes accessed | tf_op | source)
XLA Modules:
  0.0 90.6 jit_solution(9939952330552257005)
XLA Ops:
  0.7 87.9 %shard_map.82 = bf16[192,2048]{1,0:T(8,128)(2,1)} custom-call(s32[4]{0:T(128)} %counts_ref.1, f32[1]{0:T(128)S(6)} %copy.10.gate_ref, bf16[192,1024]{1,0:T(8,128)(2,1)} %q_ref.1, s32[2,192]{1,0:T(2,128)} %range_ref.1, bf16[1601,128]{1,0:T(8,128)(2,1)} %k_hbm.1, bf16[1601,128]{1,0:T(8,128)(2,1)} %v_hbm.1, bf16[1024,8192]{1,0:T(8,128)(2,1)} %w_hbm.1, ...), custom_call_target="tpu_custom_call" | custom-call | tf_op jit(solution)/shard_map/pallas_call | solution.py:538
  88.5 2.1 %copy.11 = bf16[192,2048]{1,0:T(8,128)(2,1)} copy(bf16[192,2048]{1,0:T(8,128)(2,1)} %shard_map.82) | data formatting | bytes 1572864
